TPU v7x, 32 devices: a whole 2x2x4 slice. The times are simulated.
32 devices in a mesh: section: 8 (over z, y), state: 4 (over x, core).
Axes of the slice: x: 2, y: 2, z: 4, core: 2. Of those that a mesh axis runs over, the one named last changes fastest.
Arguments:
- initial_state: float32 [32, 1024], P('state'), may hold values from -6 to 6
- state_ref: float32 [192, 32, 1024], P('section', 'state'), may hold values from -6 to 6
- state_weight: float32 [192, 32, 1024], P('section', 'state'), may hold values from 0.2 to 5
- input_matrix: bfloat16 [32, 1024, 512], P('state'), may hold values from -0.25 to 0.25
- kkt_inverse: float32 [512, 512], replicated, may hold values from -1 to 1, as said below
- input_bound: float32 [512], replicated, may hold values from 0.02 to 0.3
Outputs:
- states: float32 [192, 32, 1024], P('section', 'state')
- boxed: float32 [192, 512], P('section')
- dual_vars: float32 [192, 32, 1024], P('section', 'state')
- history: float32 [10, 2], replicated
Inputs may be any that keep to these rules, and one draw needn't show every extreme that they name: `kkt_inverse`: a symmetric matrix.
All inputs are finite; a program needn't handle non-finite values.
Results may differ from a plain program's by a relative error of at most 0.003.
Values may be sent and summed in bfloat16 or wider, within the bound.
No kernel may reach another device: no remote copies, remote signals or barrier semaphores. Data moves between devices by JAX's collectives and lax.ppermute only.
A program may use at most 128 MiB of HBM per device.

v0:
```python
import jax
import jax.numpy as jnp
from jax import lax
from jax.sharding import PartitionSpec as P

GX = 32
GY = 32
GZ = 32
ITERS = 10
diffusion = 0.15
epsilon = 1e-06


def with_halo(block, sides, width):
    for axis, dim in sides:
        count = lax.axis_size(axis)
        forward = [(i, i + 1) for i in range(count - 1)]
        backward = [(target, source) for source, target in forward]
        low = lax.ppermute(
            lax.slice_in_dim(block, block.shape[dim] - width, None, axis=dim), axis, forward
        )
        high = lax.ppermute(lax.slice_in_dim(block, 0, width, axis=dim), axis, backward)
        block = jnp.concatenate([low, block, high], axis=dim)
    return block


def passed_along(value, axis, steps):
    count = lax.axis_size(axis)
    leading, last = (max(0, -steps), min(count, count - steps))
    return lax.ppermute(value, axis, [(source, source + steps) for source in range(leading, last)])


def stencil(padded):
    centre = padded[:, 1:-1]
    across = padded[:, 2:] + padded[:, :-2]
    depth = centre.shape[-1]
    flat_pad = jnp.pad(centre, ((0, 0), (0, 0), (GZ, GZ)))
    along_y = flat_pad[:, :, 2 * GZ :] + flat_pad[:, :, : -2 * GZ]
    lower_z = jnp.pad(centre, ((0, 0), (0, 0), (1, 0)))[:, :, :-1]
    upper_z = jnp.pad(centre, ((0, 0), (0, 0), (0, 1)))[:, :, 1:]
    z_index = jnp.arange(depth) % GZ
    along_z = jnp.where(z_index > 0, lower_z, 0.0) + jnp.where(z_index < GZ - 1, upper_z, 0.0)
    return centre + diffusion * (across + along_y + along_z - 6.0 * centre)


def apply_rows(inputs_low, matrix):
    return lax.dot_general(
        inputs_low, matrix, (((1,), (1,)), ((), ())), preferred_element_type=jnp.float32
    )


def local(initial_state, state_ref, state_weight, input_matrix, kkt_inverse, input_bound):
    section_count, planes, plane_size = state_ref.shape
    input_width = input_matrix.shape[2]
    matrix = input_matrix.reshape(planes * plane_size, input_width)
    penalty = float(GX * GY * GZ) / input_width
    is_first = lax.axis_index("section") == 0
    groups = lax.axis_size("state")
    state_seat = lax.axis_index("state")
    cell_count = section_count * lax.axis_size("section") * GX * GY * GZ
    input_count = section_count * lax.axis_size("section") * input_width
    states = jnp.zeros_like(state_ref)
    dual_vars = jnp.zeros_like(state_ref)
    boxed = jnp.zeros((section_count, input_width), jnp.float32)
    scaled = jnp.zeros((section_count, input_width), jnp.float32)
    wide_matrix = with_halo(input_matrix, (("state", 0),), 1).reshape(-1, input_width)
    plane_index = jnp.arange(planes + 2)[:, None]
    outside = (plane_index == 0) & (state_seat == 0) | (plane_index == planes + 1) & (
        state_seat == groups - 1
    )
    rim_mask = jnp.where(outside, 0.0, 1.0).astype(jnp.float32)
    history = []
    for iteration in range(ITERS):
        last_state = passed_along(states[-1], "section", 1)
        prior = jnp.where(is_first, initial_state, last_state)
        joined = jnp.concatenate([prior[None], states, dual_vars], 0)
        padded = with_halo(joined, (("state", 1),), 2)
        moved_wide = stencil(padded[:section_count])
        states_wide = padded[1 : section_count + 1, 1:-1]
        duals_wide = padded[section_count + 1 :, 1:-1]
        target_wide = states_wide - moved_wide + duals_wide
        moved_prior = moved_wide[:, 1:-1]
        target = target_wide[:, 1:-1]
        target_low = target.astype(jnp.bfloat16).reshape(section_count, -1)
        partial_pull = jnp.dot(target_low, matrix, preferred_element_type=jnp.float32)
        pulled = lax.psum(partial_pull, "state")
        rhs_rows = pulled + penalty * (boxed - scaled)
        inputs = jnp.dot(rhs_rows, kkt_inverse, precision=lax.Precision.HIGHEST)
        inputs_low = inputs.astype(jnp.bfloat16)
        driven_wide = apply_rows(inputs_low, wide_matrix).reshape(
            section_count, planes + 2, plane_size
        )
        defect_wide = (target_wide - driven_wide) * rim_mask
        driven = driven_wide[:, 1:-1]
        defect = defect_wide[:, 1:-1]
        following = passed_along(defect_wide[0], "section", -1)
        ahead_defect = jnp.concatenate([defect_wide[1:], following[None]], 0)
        back_term = stencil(ahead_defect)
        updated = (state_weight * state_ref + (states - defect) + back_term + states) / (
            state_weight + 2.0
        )
        primal = updated - moved_prior - driven
        dual_vars = dual_vars + primal
        boxed_new = jnp.clip(inputs + scaled, -input_bound, input_bound)
        box_gap = inputs - boxed_new
        scaled = scaled + box_gap
        boxed = boxed_new
        states = updated
        primal_square = jnp.sum(primal * primal)
        gap_square = jnp.sum(box_gap * box_gap) / groups
        totals = lax.psum((primal_square, gap_square), ("section", "state"))
        history.append(
            jnp.stack(
                [
                    jnp.sqrt(totals[0] / cell_count + epsilon),
                    jnp.sqrt(totals[1] / input_count + epsilon),
                ]
            )
        )
    record = jnp.stack(history)
    return (states, boxed, dual_vars, record)


def solution(mesh):
    return jax.shard_map(
        local,
        mesh=mesh,
        in_specs=(
            P("state", None),
            P("section", "state", None),
            P("section", "state", None),
            P("state", None, None),
            P(),
            P(),
        ),
        out_specs=(
            P("section", "state", None),
            P("section", None),
            P("section", "state", None),
            P(),
        ),
        check_vma=False,
    )
```

profile of v0, /device:TPU:12, one launch (start us, length us, event | category | flops | bytes accessed | tf_op | source)
XLA Modules:
  0.0 624.9 jit_solution(1933036389020178397)
XLA Ops:
  0.7 3.6 collective-permute-start
  14.2 4.0 collective-permute-start.3
  25.3 14.3 %psum.210 = f32[24,512]{1,0:T(8,128)S(1)} all-reduce(f32[24,512]{1,0:T(8,128)S(1)} %convolution_bitcast_fusion.9), channel_id=1, replica_groups=mesh['section'=8,'state'=4] {'state'}, use_global_device_ids=true, to_apply=%region_0.1 | all-reduce | flops 12288 | bytes 98304 | tf_op jit(solution)/shard_map/psum | solution.py:86
  42.5 7.3 %constant_dynamic-update-slice_fusion.1 = bf16[10,1024,512]{2,1,0:T(8,128)(2,1)} fusion(bf16[10,1024,512]{2,1,0:T(8,128)(2,1)} %constant_dynamic-update-slice_fusion.2, bf16[8,1024,512]{2,1,0:T(8,128)(2,1)} %param.9), kind=kLoop, calls=%fused_computation.746 | loop fusion | bytes 16777216
  52.1 6.9 %fusion.342 = f32[24,10,1024]{2,0,1:T(8,128)S(1)} fusion(bf16[10,1024,512]{2,1,0:T(8,128)(2,1)} %constant_dynamic-update-slice_fusion, f32[24,512]{1,0:T(8,128)S(1)} %fusion.421), kind=kOutput, calls=%fused_computation.705 | convolution fusion | flops 251670528 | bytes 11517952 | tf_op jit(solution)/shard_map/dot_general | solution.py:47
  59.9 3.3 collective-permute-start.5
  69.3 3.6 collective-permute-start.6
  82.0 3.3 slice_add_fusion.3
  88.2 16.2 %psum.211 = f32[24,512]{1,0:T(8,128)} all-reduce(f32[24,512]{1,0:T(8,128)S(1)} %convolution_bitcast_fusion.8), channel_id=1, replica_groups=mesh['section'=8,'state'=4] {'state'}, use_global_device_ids=true, to_apply=%region_1.2 | all-reduce | flops 12288 | bytes 98304 | tf_op jit(solution)/shard_map/psum | solution.py:86
  106.4 6.9 %fusion.340 = f32[24,10,1024]{2,0,1:T(8,128)S(1)} fusion(bf16[10,1024,512]{2,1,0:T(8,128)(2,1)} %constant_dynamic-update-slice_fusion, f32[24,512]{1,0:T(8,128)S(1)} %get-tuple-element.121), kind=kOutput, calls=%fused_computation.703 | convolution fusion | flops 251670528 | bytes 11517952 | tf_op jit(solution)/shard_map/dot_general | solution.py:47
  114.3 3.3 collective-permute-start.9
  117.8 3.9 collective-permute-done.9
  124.7 3.4 collective-permute-start.10
  132.1 3.5 collective-permute-start.11
  137.3 3.3 slice_add_fusion.2
  143.5 15.6 %psum.212 = f32[24,512]{1,0:T(8,128)S(1)} all-reduce(f32[24,512]{1,0:T(8,128)S(1)} %convolution_bitcast_fusion.7), channel_id=1, replica_groups=mesh['section'=8,'state'=4] {'state'}, use_global_device_ids=true, to_apply=%region_2.3 | all-reduce | flops 12288 | bytes 98304 | tf_op jit(solution)/shard_map/psum | solution.py:86
  159.8 6.9 %fusion.338 = f32[24,10,1024]{2,0,1:T(8,128)S(1)} fusion(bf16[10,1024,512]{2,1,0:T(8,128)(2,1)} %constant_dynamic-update-slice_fusion, f32[24,512]{1,0:T(8,128)S(1)} %fusion.297), kind=kOutput, calls=%fused_computation.701 | convolution fusion | flops 251670528 | bytes 11517952 | tf_op jit(solution)/shard_map/dot_general | solution.py:47
  167.6 3.3 collective-permute-start.13
  171.1 3.9 collective-permute-done.13
  178.0 3.4 collective-permute-start.14
  185.4 3.2 collective-permute-start.15
  190.7 3.3 slice_add_fusion.1
  197.5 16.8 %psum.213 = f32[24,512]{1,0:T(8,128)} all-reduce(f32[24,512]{1,0:T(8,128)} %convolution_bitcast_fusion.6), channel_id=1, replica_groups=mesh['section'=8,'state'=4] {'state'}, use_global_device_ids=true, to_apply=%region_3.4 | all-reduce | flops 12288 | bytes 98304 | tf_op jit(solution)/shard_map/psum | solution.py:86
  216.3 6.9 %fusion.336 = f32[24,10,1024]{2,0,1:T(8,128)S(1)} fusion(bf16[10,1024,512]{2,1,0:T(8,128)(2,1)} %constant_dynamic-update-slice_fusion, f32[24,512]{1,0:T(8,128)S(1)} %get-tuple-element.123), kind=kOutput, calls=%fused_computation.699 | convolution fusion | flops 251670528 | bytes 11517952 | tf_op jit(solution)/shard_map/dot_general | solution.py:47
  224.2 3.3 collective-permute-start.17
  227.7 3.9 collective-permute-done.17
  234.5 3.4 collective-permute-start.18
  241.9 3.3 collective-permute-start.19
  247.2 3.3 slice_add_fusion
  253.3 15.6 %psum.214 = f32[24,512]{1,0:T(8,128)S(1)} all-reduce(f32[24,512]{1,0:T(8,128)S(1)} %convolution_bitcast_fusion.5), channel_id=1, replica_groups=mesh['section'=8,'state'=4] {'state'}, use_global_device_ids=true, to_apply=%region_4.5 | all-reduce | flops 12288 | bytes 98304 | tf_op jit(solution)/shard_map/psum | solution.py:86
  269.6 6.9 %fusion.334 = f32[24,10,1024]{2,0,1:T(8,128)S(1)} fusion(bf16[10,1024,512]{2,1,0:T(8,128)(2,1)} %constant_dynamic-update-slice_fusion, f32[24,512]{1,0:T(8,128)S(1)} %fusion.289), kind=kOutput, calls=%fused_computation.697 | convolution fusion | flops 251670528 | bytes 11517952 | tf_op jit(solution)/shard_map/dot_general | solution.py:47
  277.4 3.3 collective-permute-start.21
  280.9 3.9 collective-permute-done.21
  289.3 3.4 collective-permute-start.22
  296.6 3.7 collective-permute-start.23
  306.1 17.3 %psum.215 = f32[24,512]{1,0:T(8,128)} all-reduce(f32[24,512]{1,0:T(8,128)} %convolution_bitcast_fusion.4), channel_id=1, replica_groups=mesh['section'=8,'state'=4] {'state'}, use_global_device_ids=true, to_apply=%region_5.6 | all-reduce | flops 12288 | bytes 98304 | tf_op jit(solution)/shard_map/psum | solution.py:86
  325.6 7.6 %subtract_multiply_fusion.8 = (f32[24,10,1024]{2,0,1:T(8,128)S(1)}, f32[24,10,1024]{2,0,1:T(8,128)S(1)}) fusion(f32[10]{0:T(128)} %copy-done.88, f32[49,12,1024]{2,0,1:T(8,128)} %copy-done.33, f32[24,10,1024]{2,0,1:T(8,128)S(1)} %copy-done.7, bf16[10,1024,512]{2,1,0:T(8,128)(2,1)} %constant_dynamic-update-slice_fusion, f32[24,512]{1,0:T(8,128)S(1)} %get-tuple-element.127), kind=kOutput, calls=%fused_computation.278 | convolution fusion | flops 252653568 | bytes 15450152 | tf_op jit(solution)/shard_map/dot_general | solution.py:47
  333.2 3.4 collective-permute-start.25
  336.8 4.0 collective-permute-done.25
  343.3 3.4 collective-permute-start.26
  350.6 3.3 collective-permute-start.27
  359.6 16.3 %psum.216 = f32[24,512]{1,0:T(8,128)S(1)} all-reduce(f32[24,512]{1,0:T(8,128)S(1)} %convolution_bitcast_fusion.3), channel_id=1, replica_groups=mesh['section'=8,'state'=4] {'state'}, use_global_device_ids=true, to_apply=%region_6.7 | all-reduce | flops 12288 | bytes 98304 | tf_op jit(solution)/shard_map/psum | solution.py:86
  377.2 7.5 %subtract_multiply_fusion.7 = (f32[24,10,1024]{2,0,1:T(8,128)S(1)}, f32[24,10,1024]{2,0,1:T(8,128)S(1)}) fusion(f32[10]{0:T(128)S(1)} %copy-done.93, f32[49,12,1024]{2,0,1:T(8,128)} %copy-done.35, f32[24,10,1024]{2,0,1:T(8,128)S(1)} %copy-done.11, bf16[10,1024,512]{2,1,0:T(8,128)(2,1)} %constant_dynamic-update-slice_fusion, f32[24,512]{1,0:T(8,128)S(1)} %fusion.281), kind=kOutput, calls=%fused_computation.277 | convolution fusion | flops 252653568 | bytes 15450152 | tf_op jit(solution)/shard_map/dot_general | solution.py:47
  384.8 3.4 collective-permute-start.29
  388.4 3.9 collective-permute-done.29
  394.6 3.4 collective-permute-start.30
  401.9 3.3 collective-permute-start.31
  411.5 17.3 %psum.217 = f32[24,512]{1,0:T(8,128)} all-reduce(f32[24,512]{1,0:T(8,128)} %convolution_bitcast_fusion.2), channel_id=1, replica_groups=mesh['section'=8,'state'=4] {'state'}, use_global_device_ids=true, to_apply=%region_7.8 | all-reduce | flops 12288 | bytes 98304 | tf_op jit(solution)/shard_map/psum | solution.py:86
  431.0 7.6 %subtract_multiply_fusion.6 = (f32[24,10,1024]{2,0,1:T(8,128)S(1)}, f32[24,10,1024]{2,0,1:T(8,128)S(1)}) fusion(f32[10]{0:T(128)} %copy-done.88, f32[49,12,1024]{2,0,1:T(8,128)} %copy-done.34, f32[24,10,1024]{2,0,1:T(8,128)S(1)} %copy-done.9, bf16[10,1024,512]{2,1,0:T(8,128)(2,1)} %constant_dynamic-update-slice_fusion, f32[24,512]{1,0:T(8,128)S(1)} %get-tuple-element.133), kind=kOutput, calls=%fused_computation.276 | convolution fusion | flops 252653568 | bytes 15450152 | tf_op jit(solution)/shard_map/dot_general | solution.py:47
  438.6 3.3 collective-permute-start.33
  442.0 4.0 collective-permute-done.33
  448.3 3.6 collective-permute-start.34
  455.9 3.1 collective-permute-start.35
  464.6 16.2 %psum.218 = f32[24,512]{1,0:T(8,128)S(1)} all-reduce(f32[24,512]{1,0:T(8,128)S(1)} %convolution_bitcast_fusion.1), channel_id=1, replica_groups=mesh['section'=8,'state'=4] {'state'}, use_global_device_ids=true, to_apply=%region_8.9 | all-reduce | flops 12288 | bytes 98304 | tf_op jit(solution)/shard_map/psum | solution.py:86
  482.0 7.5 %subtract_multiply_fusion.5 = (f32[24,10,1024]{2,0,1:T(8,128)S(1)}, f32[24,10,1024]{2,0,1:T(8,128)S(1)}) fusion(f32[10]{0:T(128)S(1)} %copy-done.94, f32[49,12,1024]{2,0,1:T(8,128)} %copy-done.36, f32[24,10,1024]{2,0,1:T(8,128)S(1)} %copy-done.13, bf16[10,1024,512]{2,1,0:T(8,128)(2,1)} %constant_dynamic-update-slice_fusion, f32[24,512]{1,0:T(8,128)S(1)} %fusion.273), kind=kOutput, calls=%fused_computation.275 | convolution fusion | flops 252653568 | bytes 15450152 | tf_op jit(solution)/shard_map/dot_general | solution.py:47
  489.6 3.4 collective-permute-start.37
  493.1 4.0 collective-permute-done.37
  499.4 3.4 collective-permute-start.38
  516.2 17.7 %psum.219 = f32[24,512]{1,0:T(8,128)} all-reduce(f32[24,512]{1,0:T(8,128)} %convolution_bitcast_fusion), channel_id=1, replica_groups=mesh['section'=8,'state'=4] {'state'}, use_global_device_ids=true, to_apply=%region_9.10 | all-reduce | flops 12288 | bytes 98304 | tf_op jit(solution)/shard_map/psum | solution.py:86
  533.8 3.2 multiply_reduce_fusion.12
  537.0 8.5 %subtract_multiply_fusion.4 = (f32[24,10,1024]{2,0,1:T(8,128)S(1)}, f32[24,10,1024]{2,0,1:T(8,128)}) fusion(f32[10]{0:T(128)S(1)} %copy-done.95, f32[49,12,1024]{2,0,1:T(8,128)} %copy-done.37, f32[24,10,1024]{2,0,1:T(8,128)S(1)} %copy-done.15, bf16[10,1024,512]{2,1,0:T(8,128)(2,1)} %constant_dynamic-update-slice_fusion, ...), kind=kOutput, calls=%fused_computation.274 | convolution fusion | flops 252641280 | bytes 15425576 | tf_op jit(solution)/shard_map/dot_general | solution.py:47
  545.5 3.3 collective-permute-start.41
  558.3 3.8 multiply_reduce_fusion
  565.0 43.7 %all-reduce.61 = (f32[]{:T(128)}, f32[]{:T(128)}, f32[]{:T(128)}, f32[]{:T(128)}, f32[]{:T(128)}, /*index=5*/f32[]{:T(128)}, f32[]{:T(128)}, f32[]{:T(128)}, f32...) all-reduce(f32[]{:T(128)S(6)} %div.131, ...), channel_id=1, replica_groups=mesh['section'=8,'state'=4] {'section','state'}, use_global_device_ids=true, to_apply=%region_13.14 | all-reduce | flops 20 | bytes 160 | tf_op jit(solution)/shard_map/psum | solution.py:111
  (480 shorter events, 166.9 us)
Async XLA Ops:
  0.6 39.0 %copy-start = (f32[512,512]{1,0:T(8,128)S(1)}, f32[512,512]{1,0:T(8,128)}, u32[]{:S(2)}) copy-start(f32[512,512]{1,0:T(8,128)} %param.10) | copy-start | bytes 3145732
  0.7 5.9 collective-permute-start
  6.8 12.9 %collective-permute-start.2 = (f32[49,2,1024]{2,1,0:T(2,128)S(1)}, f32[49,2,1024]{2,1,0:T(2,128)S(1)}, u32[]{:S(2)}, u32[]{:S(2)}) collective-permute-start(f32[49,2,1024]{2,1,0:T(2,128)S(1)} %get-tuple-element.119), channel_id=1, source_target_pairs={{1,0},{2,1},{3,2},{5,4},{6,5},{7,6},{9,8},{10,9},{11,10},{13,12},{... | collective-permute-start | bytes 1204232 | tf_op jit(solution)/shard_map/ppermute | solution.py:22
  8.1 11.6 %collective-permute-start.1 = (f32[49,2,1024]{2,1,0:T(2,128)S(1)}, f32[49,2,1024]{2,1,0:T(2,128)S(1)}, u32[]{:S(2)}, u32[]{:S(2)}) collective-permute-start(f32[49,2,1024]{2,1,0:T(2,128)S(1)} %get-tuple-element.118), channel_id=1, source_target_pairs={{0,1},{1,2},{2,3},{4,5},{5,6},{6,7},{8,9},{9,10},{10,11},{12,13},{... | collective-permute-start | bytes 1204232 | tf_op jit(solution)/shard_map/ppermute | solution.py:19
  14.2 26.1 %collective-permute-start.3 = (bf16[1,1024,512]{2,1,0:T(8,128)(2,1)}, bf16[1,1024,512]{2,1,0:T(8,128)(2,1)}, u32[]{:S(2)}, u32[]{:S(2)}) collective-permute-start(bf16[1,1024,512]{2,1,0:T(8,128)(2,1)} %get-tuple-element.86), channel_id=1, source_target_pairs={{0,1},{1,2},{2,3},{4,5},{5,6},{6,7},{8,9},{9,10},{10,11},{12,13},{... | collective-permute-start | bytes 3145736 | tf_op jit(solution)/shard_map/ppermute | solution.py:19
  18.2 31.6 %collective-permute-start.4 = (bf16[1,1024,512]{2,1,0:T(8,128)(2,1)}, bf16[1,1024,512]{2,1,0:T(8,128)(2,1)}, u32[]{:S(2)}, u32[]{:S(2)}) collective-permute-start(bf16[1,1024,512]{2,1,0:T(8,128)(2,1)} %get-tuple-element.85), channel_id=1, source_target_pairs={{1,0},{2,1},{3,2},{5,4},{6,5},{7,6},{9,8},{10,9},{11,10},{13,12},{... | collective-permute-start | bytes 3145736 | tf_op jit(solution)/shard_map/ppermute | solution.py:22
  19.5 39.5 %copy-start.88 = (f32[10]{0:T(128)}, f32[10]{0:T(128)S(1)}, u32[]{:S(2)}) copy-start(f32[10]{0:T(128)S(1)} %or_select_fusion) | copy-start | bytes 124
  59.9 7.5 %collective-permute-start.5 = (f32[10,1024]{1,0:T(8,128)S(1)}, f32[10,1024]{1,0:T(8,128)S(1)}, u32[]{:S(2)}, u32[]{:S(2)}) collective-permute-start(f32[10,1024]{1,0:T(8,128)S(1)} %slice_bitcast_fusion.4), channel_id=1, source_target_pairs={{4,0},{8,4},{12,8},{16,12},{20,16},{24,20},{28,24},{5,1},{9,5},{13... | collective-permute-start | bytes 122888 | tf_op jit(solution)/shard_map/ppermute | solution.py:30
  69.3 5.8 collective-permute-start.6
  75.4 4.4 collective-permute-start.8
  76.7 4.4 collective-permute-start.7
  114.3 7.4 %collective-permute-start.9 = (f32[10,1024]{1,0:T(8,128)S(1)}, f32[10,1024]{1,0:T(8,128)S(1)}, u32[]{:S(2)}, u32[]{:S(2)}) collective-permute-start(f32[10,1024]{1,0:T(8,128)S(1)} %slice_bitcast_fusion.3), channel_id=1, source_target_pairs={{4,0},{8,4},{12,8},{16,12},{20,16},{24,20},{28,24},{5,1},{9,5},{13... | collective-permute-start | bytes 122888 | tf_op jit(solution)/shard_map/ppermute | solution.py:30
  124.7 5.8 collective-permute-start.10
  130.8 4.8 collective-permute-start.12
  132.1 4.4 collective-permute-start.11
  142.0 17.1 %copy-start.66 = (f32[24,512]{1,0:T(8,128)S(1)}, f32[24,512]{1,0:T(8,128)}, u32[]{:S(2)}) copy-start(f32[24,512]{1,0:T(8,128)} %get-tuple-element.120) | copy-start | bytes 147460
  142.0 17.1 %copy-start.77 = (f32[24,512]{1,0:T(8,128)S(1)}, f32[24,512]{1,0:T(8,128)}, u32[]{:S(2)}) copy-start(f32[24,512]{1,0:T(8,128)} %copy-done.76) | copy-start | bytes 147460
  167.6 7.4 %collective-permute-start.13 = (f32[10,1024]{1,0:T(8,128)S(1)}, f32[10,1024]{1,0:T(8,128)S(1)}, u32[]{:S(2)}, u32[]{:S(2)}) collective-permute-start(f32[10,1024]{1,0:T(8,128)S(1)} %slice_bitcast_fusion.2), channel_id=1, source_target_pairs={{4,0},{8,4},{12,8},{16,12},{20,16},{24,20},{28,24},{5,1},{9,5},{13... | collective-permute-start | bytes 122888 | tf_op jit(solution)/shard_map/ppermute | solution.py:30
  178.0 5.8 collective-permute-start.14
  184.1 4.5 collective-permute-start.16
  185.4 4.4 collective-permute-start.15
  224.2 7.4 %collective-permute-start.17 = (f32[10,1024]{1,0:T(8,128)S(1)}, f32[10,1024]{1,0:T(8,128)S(1)}, u32[]{:S(2)}, u32[]{:S(2)}) collective-permute-start(f32[10,1024]{1,0:T(8,128)S(1)} %slice_bitcast_fusion.1), channel_id=1, source_target_pairs={{4,0},{8,4},{12,8},{16,12},{20,16},{24,20},{28,24},{5,1},{9,5},{13... | collective-permute-start | bytes 122888 | tf_op jit(solution)/shard_map/ppermute | solution.py:30
  234.5 5.8 collective-permute-start.18
  240.6 4.6 collective-permute-start.20
  241.9 4.4 collective-permute-start.19
  251.8 17.1 %copy-start.67 = (f32[24,512]{1,0:T(8,128)S(1)}, f32[24,512]{1,0:T(8,128)}, u32[]{:S(2)}) copy-start(f32[24,512]{1,0:T(8,128)} %get-tuple-element.120) | copy-start | bytes 147460
  251.8 17.1 %copy-start.72 = (f32[24,512]{1,0:T(8,128)S(1)}, f32[24,512]{1,0:T(8,128)}, u32[]{:S(2)}) copy-start(f32[24,512]{1,0:T(8,128)} %get-tuple-element.122) | copy-start | bytes 147460
  251.8 17.1 %copy-start.79 = (f32[24,512]{1,0:T(8,128)S(1)}, f32[24,512]{1,0:T(8,128)}, u32[]{:S(2)}) copy-start(f32[24,512]{1,0:T(8,128)} %copy-done.78) | copy-start | bytes 147460
  277.4 7.4 %collective-permute-start.21 = (f32[10,1024]{1,0:T(8,128)S(1)}, f32[10,1024]{1,0:T(8,128)S(1)}, u32[]{:S(2)}, u32[]{:S(2)}) collective-permute-start(f32[10,1024]{1,0:T(8,128)S(1)} %slice_bitcast_fusion), channel_id=1, source_target_pairs={{4,0},{8,4},{12,8},{16,12},{20,16},{24,20},{28,24},{5,1},{9,5},{13... | collective-permute-start | bytes 122888 | tf_op jit(solution)/shard_map/ppermute | solution.py:30
  289.3 5.8 collective-permute-start.22
  295.3 5.1 collective-permute-start.24
  296.6 4.7 collective-permute-start.23
  333.2 7.6 %collective-permute-start.25 = (f32[10,1024]{1,0:T(8,128)S(1)}, f32[10,1024]{1,0:T(8,128)S(1)}, u32[]{:S(2)}, u32[]{:S(2)}) collective-permute-start(f32[10,1024]{1,0:T(8,128)S(1)} %bitcast.237), channel_id=1, source_target_pairs={{4,0},{8,4},{12,8},{16,12},{20,16},{24,20},{28,24},{5,1},{9,5},{13... | collective-permute-start | bytes 122888 | tf_op jit(solution)/shard_map/ppermute | solution.py:30
  343.3 12.7 %copy-start.2 = (f32[24,8,1024]{2,0,1:T(8,128)}, f32[24,8,1024]{2,0,1:T(8,128)S(1)}, u32[]{:S(2)}) copy-start(f32[24,8,1024]{2,0,1:T(8,128)S(1)} %get-tuple-element.59) | copy-start | bytes 2359300
  343.3 5.8 collective-permute-start.26
  349.3 4.6 collective-permute-start.28
  350.6 4.7 collective-permute-start.27
  358.3 17.6 %copy-start.69 = (f32[24,512]{1,0:T(8,128)S(1)}, f32[24,512]{1,0:T(8,128)}, u32[]{:S(2)}) copy-start(f32[24,512]{1,0:T(8,128)} %copy-done.68) | copy-start | bytes 147460
  358.3 17.6 %copy-start.73 = (f32[24,512]{1,0:T(8,128)S(1)}, f32[24,512]{1,0:T(8,128)}, u32[]{:S(2)}) copy-start(f32[24,512]{1,0:T(8,128)} %get-tuple-element.122) | copy-start | bytes 147460
  358.4 17.6 %copy-start.74 = (f32[24,512]{1,0:T(8,128)S(1)}, f32[24,512]{1,0:T(8,128)}, u32[]{:S(2)}) copy-start(f32[24,512]{1,0:T(8,128)} %get-tuple-element.126) | copy-start | bytes 147460
  358.4 17.6 %copy-start.81 = (f32[24,512]{1,0:T(8,128)S(1)}, f32[24,512]{1,0:T(8,128)}, u32[]{:S(2)}) copy-start(f32[24,512]{1,0:T(8,128)} %copy-done.80) | copy-start | bytes 147460
  358.4 18.3 %copy-start.93 = (f32[10]{0:T(128)S(1)}, f32[10]{0:T(128)}, u32[]{:S(2)}) copy-start(f32[10]{0:T(128)} %copy-done.88) | copy-start | bytes 124
  384.8 7.5 %collective-permute-start.29 = (f32[10,1024]{1,0:T(8,128)S(1)}, f32[10,1024]{1,0:T(8,128)S(1)}, u32[]{:S(2)}, u32[]{:S(2)}) collective-permute-start(f32[10,1024]{1,0:T(8,128)S(1)} %bitcast.239), channel_id=1, source_target_pairs={{4,0},{8,4},{12,8},{16,12},{20,16},{24,20},{28,24},{5,1},{9,5},{13... | collective-permute-start | bytes 122888 | tf_op jit(solution)/shard_map/ppermute | solution.py:30
  394.6 5.8 collective-permute-start.30
  400.6 4.6 collective-permute-start.32
  401.9 4.7 collective-permute-start.31
  438.6 7.4 %collective-permute-start.33 = (f32[10,1024]{1,0:T(8,128)S(1)}, f32[10,1024]{1,0:T(8,128)S(1)}, u32[]{:S(2)}, u32[]{:S(2)}) collective-permute-start(f32[10,1024]{1,0:T(8,128)S(1)} %bitcast.241), channel_id=1, source_target_pairs={{4,0},{8,4},{12,8},{16,12},{20,16},{24,20},{28,24},{5,1},{9,5},{13... | collective-permute-start | bytes 122888 | tf_op jit(solution)/shard_map/ppermute | solution.py:30
  446.2 17.1 %slice-start.16 = ((s8[8388608]{0:T(1024)(128)(4,1)}), s8[4194304]{0:T(1024)(128)(4,1)S(1)}, s32[]{:S(2)}) async-start(s8[8388608]{0:T(1024)(128)(4,1)} %bitcast.222), calls=%async_computation.16 | async-start | bytes 8388608
  448.2 12.7 %copy-start.4 = (f32[24,8,1024]{2,0,1:T(8,128)}, f32[24,8,1024]{2,0,1:T(8,128)S(1)}, u32[]{:S(2)}) copy-start(f32[24,8,1024]{2,0,1:T(8,128)S(1)} %get-tuple-element.55) | copy-start | bytes 2359300
  448.3 5.8 collective-permute-start.34
  454.3 4.6 collective-permute-start.36
  455.9 4.5 collective-permute-start.35
  463.3 17.5 %copy-start.71 = (f32[24,512]{1,0:T(8,128)S(1)}, f32[24,512]{1,0:T(8,128)}, u32[]{:S(2)}) copy-start(f32[24,512]{1,0:T(8,128)} %copy-done.70) | copy-start | bytes 147460
  463.3 17.5 %copy-start.75 = (f32[24,512]{1,0:T(8,128)S(1)}, f32[24,512]{1,0:T(8,128)}, u32[]{:S(2)}) copy-start(f32[24,512]{1,0:T(8,128)} %get-tuple-element.126) | copy-start | bytes 147460
  463.3 17.5 %copy-start.83 = (f32[24,512]{1,0:T(8,128)S(1)}, f32[24,512]{1,0:T(8,128)}, u32[]{:S(2)}) copy-start(f32[24,512]{1,0:T(8,128)} %copy-done.82) | copy-start | bytes 147460
  463.3 17.5 %copy-start.86 = (f32[24,512]{1,0:T(8,128)S(1)}, f32[24,512]{1,0:T(8,128)}, u32[]{:S(2)}) copy-start(f32[24,512]{1,0:T(8,128)} %get-tuple-element.132) | copy-start | bytes 147460
  463.3 18.1 %copy-start.94 = (f32[10]{0:T(128)S(1)}, f32[10]{0:T(128)}, u32[]{:S(2)}) copy-start(f32[10]{0:T(128)} %copy-done.88) | copy-start | bytes 124
  489.6 7.5 %collective-permute-start.37 = (f32[10,1024]{1,0:T(8,128)S(1)}, f32[10,1024]{1,0:T(8,128)S(1)}, u32[]{:S(2)}, u32[]{:S(2)}) collective-permute-start(f32[10,1024]{1,0:T(8,128)S(1)} %bitcast.243), channel_id=1, source_target_pairs={{4,0},{8,4},{12,8},{16,12},{20,16},{24,20},{28,24},{5,1},{9,5},{13... | collective-permute-start | bytes 122888 | tf_op jit(solution)/shard_map/ppermute | solution.py:30
  497.3 17.1 %slice-start.18 = ((s8[8388608]{0:T(1024)(128)(4,1)}), s8[4194304]{0:T(1024)(128)(4,1)S(1)}, s32[]{:S(2)}) async-start(s8[8388608]{0:T(1024)(128)(4,1)} %bitcast.224), calls=%async_computation.18 | async-start | bytes 8388608
  499.4 5.8 collective-permute-start.38
  505.4 4.6 collective-permute-start.40
  506.9 4.5 collective-permute-start.39
  516.2 20.8 %copy-start.95 = (f32[10]{0:T(128)S(1)}, f32[10]{0:T(128)}, u32[]{:S(2)}) copy-start(f32[10]{0:T(128)} %copy-done.88) | copy-start | bytes 124
  545.5 10.6 %collective-permute-start.41 = (f32[10,1024]{1,0:T(8,128)S(1)}, f32[10,1024]{1,0:T(8,128)}, u32[]{:S(2)}, u32[]{:S(2)}) collective-permute-start(f32[10,1024]{1,0:T(8,128)S(1)} %bitcast.236), channel_id=1, source_target_pairs={{4,0},{8,4},{12,8},{16,12},{20,16},{24,20},{28,24},{5,1},{9,5},{13... | collective-permute-start | bytes 122888 | tf_op jit(solution)/shard_map/ppermute | solution.py:30
  (94 other events, 467.7 us)
where the time goes:
time: 635 us; the launch traced here: 625 us
  blocking collectives  207 us (33%)
  starting transfers between devices  120 us (19%)
  matrix products  104 us (16%)
  other arithmetic  67.4 us (11%)
  waiting for transfers between devices  61.4 us (10%)
  local copies, waits for them, and re-layouts  42 us (7%)
  between operations  23.2 us (4%)
    psum x10, blocking collectives, local(): pulled = lax.psum(partial_pull, 'state')  163 us
    dot_general x10, matrix products, apply_rows(): lax.dot_general(inputs_low, matrix, (((1,), (1,)), ((), ())), preferred_e...  73.3 us
    ppermute x20, starting transfers between devices, passed_along(): lax.ppermute(value, axis, [(source, source + steps) for source in range(l...  68.3 us
    ppermute x20, waiting for transfers between devices, passed_along(): lax.ppermute(value, axis, [(source, source + steps) for source in range(l...  50.4 us
    psum x1, blocking collectives, local(): totals = lax.psum((primal_square, gap_square), ('section', 'state'))  43.7 us
    ppermute x11, starting transfers between devices, with_halo(): lax.ppermute(lax.slice_in_dim(block, block.shape[dim] - width, None, axis...  36.6 us
    unnamed x245, local copies, waits for them, and re-layouts  26.6 us
    reduce_sum x10, other arithmetic, local(): primal_square = jnp.sum(primal * primal)  23.2 us
  transfers between devices with their start and end apart: 42, of which 28 were waited for; matrix products, arithmetic and copies ran while one was open for 5% of the time, Pallas kernels for 0%

commit v1 on v0

--- a/solution.py
+++ b/solution.py
@@ -9,6 +9,12 @@
 ITERS = 10
 diffusion = 0.15
 epsilon = 1e-06
+
+
+def summed_here(shard, mesh_axis):
+    parts = lax.all_gather(shard, mesh_axis, axis=0, tiled=False)
+    total = parts.sum(axis=0)
+    return total
 
 
 def with_halo(block, sides, width):
@@ -83,7 +89,7 @@
         target = target_wide[:, 1:-1]
         target_low = target.astype(jnp.bfloat16).reshape(section_count, -1)
         partial_pull = jnp.dot(target_low, matrix, preferred_element_type=jnp.float32)
-        pulled = lax.psum(partial_pull, "state")
+        pulled = summed_here(partial_pull, "state")
         rhs_rows = pulled + penalty * (boxed - scaled)
         inputs = jnp.dot(rhs_rows, kkt_inverse, precision=lax.Precision.HIGHEST)
         inputs_low = inputs.astype(jnp.bfloat16)

time: 635 us -> 568 us (0.89)
  blocking collectives: 207 us -> 158 us
  other arithmetic: 67.4 us -> 51.9 us
  local copies, waits for them, and re-layouts: 42 us -> 29.2 us
    psum x10 -> x0, blocking collectives: 163 us -> none  [local(): pulled = lax.psum(partial_pull, 'state')]
    all_gather x0 -> x10, blocking collectives: none -> 115 us  [summed_here(): parts = lax.all_gather(shard, mesh_axis, axis=0, tiled=False)]
    add x6 -> x0, other arithmetic: 17.5 us -> none  [the longest x5 16.2 us: local(): target_wide = states_wide - moved_wide + duals_wide]
    unnamed x245 -> x237, local copies, waits for them, and re-layouts: 26.6 us -> 16.8 us
    reduce_sum x0 -> x10, other arithmetic: none -> 7.29 us  [summed_here(): total = parts.sum(axis=0)]
  transfers between devices with their start and end apart: 42 -> 42, of which waited for: 28 -> 28; matrix products, arithmetic and copies ran while one was open for 5% -> 4% of each run, Pallas kernels for 0% -> 0%
where the time goes in v1:
time: 568 us; the launch traced here: 558 us
  blocking collectives  158 us (28%)
  starting transfers between devices  120 us (21%)
  matrix products  109 us (19%)
  waiting for transfers between devices  66 us (12%)
  other arithmetic  51.9 us (9%)
  local copies, waits for them, and re-layouts  29.2 us (5%)
  between operations  23.3 us (4%)
    all_gather x10, blocking collectives, summed_here(): parts = lax.all_gather(shard, mesh_axis, axis=0, tiled=False)  115 us
    dot_general x10, matrix products, apply_rows(): lax.dot_general(inputs_low, matrix, (((1,), (1,)), ((), ())), preferred_e...  78.7 us
    ppermute x20, starting transfers between devices, passed_along(): lax.ppermute(value, axis, [(source, source + steps) for source in range(l...  69.5 us
    ppermute x20, waiting for transfers between devices, passed_along(): lax.ppermute(value, axis, [(source, source + steps) for source in range(l...  53.5 us
    psum x1, blocking collectives, local(): totals = lax.psum((primal_square, gap_square), ('section', 'state'))  43.1 us
    ppermute x11, starting transfers between devices, with_halo(): lax.ppermute(lax.slice_in_dim(block, block.shape[dim] - width, None, axis...  36.7 us
    reduce_sum x10, other arithmetic, local(): primal_square = jnp.sum(primal * primal)  22.8 us
    unnamed x237, local copies, waits for them, and re-layouts  16.8 us
  transfers between devices with their start and end apart: 42, of which 28 were waited for; matrix products, arithmetic and copies ran while one was open for 4% of the time, Pallas kernels for 0%

profile of v1, /device:TPU:12, one launch (start us, length us, event | category | flops | bytes accessed | tf_op | source)
XLA Modules:
  0.0 557.9 jit_solution(11621624884877160638)
XLA Ops:
  0.7 3.6 collective-permute-start
  8.0 3.1 collective-permute-start.1
  14.1 4.0 collective-permute-start.3
  21.6 5.0 convolution_bitcast_fusion.9
  26.6 9.5 %all-gather = f32[96,512]{1,0:T(8,128)S(1)} all-gather(f32[24,512]{1,0:T(8,128)S(1)} %convolution_bitcast_fusion.9), channel_id=2, replica_groups=mesh['section'=8,'state'=4] {'state'}, dimensions={0}, use_global_device_ids=true | all-gather | bytes 245760 | tf_op jit(solution)/shard_map/all_gather | solution.py:15
  39.0 7.3 %constant_dynamic-update-slice_fusion.1 = bf16[10,1024,512]{2,1,0:T(8,128)(2,1)} fusion(bf16[10,1024,512]{2,1,0:T(8,128)(2,1)} %constant_dynamic-update-slice_fusion.2, bf16[8,1024,512]{2,1,0:T(8,128)(2,1)} %param.9), kind=kLoop, calls=%fused_computation.736 | loop fusion | bytes 16777216
  48.6 7.5 %subtract_multiply_fusion.9 = (f32[24,10,1024]{2,0,1:T(8,128)S(1)}, f32[24,10,1024]{2,0,1:T(8,128)S(1)}) fusion(f32[10]{0:T(128)S(1)} %or_select_fusion, f32[49,12,1024]{2,0,1:T(8,128)} %copy-done.48, f32[24,10,1024]{2,0,1:T(8,128)S(1)} %fusion.5, bf16[10,1024,512]{2,1,0:T(8,128)(2,1)} %constant_dynamic-update-slice_fusion, f32[24,512]{1,0:T(8,128)S(1)} %fusion.421), kind=kOutput, calls=%fused_computation.267 | convolution fusion | flops 252653568 | bytes 15450152 | tf_op jit(solution)/shard_map/dot_general | solution.py:53
  56.2 3.4 collective-permute-start.5
  59.7 3.7 collective-permute-done.5
  66.0 3.4 collective-permute-start.6
  81.1 11.2 %all-gather.1 = f32[96,512]{1,0:T(8,128)} all-gather(f32[24,512]{1,0:T(8,128)S(1)} %convolution_bitcast_fusion.8), channel_id=3, replica_groups=mesh['section'=8,'state'=4] {'state'}, dimensions={0}, use_global_device_ids=true | all-gather | bytes 245760 | tf_op jit(solution)/shard_map/all_gather | solution.py:15
  94.4 7.8 %subtract_multiply_fusion.8 = (f32[24,10,1024]{2,0,1:T(8,128)S(1)}, f32[24,10,1024]{2,0,1:T(8,128)S(1)}) fusion(f32[10]{0:T(128)} %copy-done.83, f32[49,12,1024]{2,0,1:T(8,128)} %copy-done.49, f32[24,10,1024]{2,0,1:T(8,128)} %copy-done.10, bf16[10,1024,512]{2,1,0:T(8,128)(2,1)} %constant_dynamic-update-slice_fusion, f32[24,512]{1,0:T(8,128)S(1)} %get-tuple-element.105), kind=kOutput, calls=%fused_computation.266 | convolution fusion | flops 252653568 | bytes 15450152 | tf_op jit(solution)/shard_map/dot_general | solution.py:53
  102.3 3.4 collective-permute-start.9
  105.9 3.7 collective-permute-done.9
  111.9 3.4 collective-permute-start.10
  119.2 3.3 collective-permute-start.11
  127.3 11.6 %all-gather.2 = f32[96,512]{1,0:T(8,128)S(1)} all-gather(f32[24,512]{1,0:T(8,128)S(1)} %convolution_bitcast_fusion.7), channel_id=4, replica_groups=mesh['section'=8,'state'=4] {'state'}, dimensions={0}, use_global_device_ids=true | all-gather | bytes 245760 | tf_op jit(solution)/shard_map/all_gather | solution.py:15
  139.6 7.8 %subtract_multiply_fusion.7 = (f32[24,10,1024]{2,0,1:T(8,128)S(1)}, f32[24,10,1024]{2,0,1:T(8,128)S(1)}) fusion(f32[10]{0:T(128)S(1)} %copy-done.84, f32[49,12,1024]{2,0,1:T(8,128)} %copy-done.53, f32[24,10,1024]{2,0,1:T(8,128)} %copy-done.18, bf16[10,1024,512]{2,1,0:T(8,128)(2,1)} %constant_dynamic-update-slice_fusion, f32[24,512]{1,0:T(8,128)S(1)} %fusion.297), kind=kOutput, calls=%fused_computation.265 | convolution fusion | flops 252653568 | bytes 15450152 | tf_op jit(solution)/shard_map/dot_general | solution.py:53
  147.4 3.4 collective-permute-start.13
  151.0 3.7 collective-permute-done.13
  156.9 3.6 collective-permute-start.14
  164.2 3.3 collective-permute-start.15
  172.2 12.0 %all-gather.3 = f32[96,512]{1,0:T(8,128)} all-gather(f32[24,512]{1,0:T(8,128)S(1)} %convolution_bitcast_fusion.6), channel_id=5, replica_groups=mesh['section'=8,'state'=4] {'state'}, dimensions={0}, use_global_device_ids=true | all-gather | bytes 245760 | tf_op jit(solution)/shard_map/all_gather | solution.py:15
  187.9 7.8 %subtract_multiply_fusion.6 = (f32[24,10,1024]{2,0,1:T(8,128)S(1)}, f32[24,10,1024]{2,0,1:T(8,128)S(1)}) fusion(f32[10]{0:T(128)} %copy-done.83, f32[49,12,1024]{2,0,1:T(8,128)} %copy-done.50, f32[24,10,1024]{2,0,1:T(8,128)} %copy-done.12, bf16[10,1024,512]{2,1,0:T(8,128)(2,1)} %constant_dynamic-update-slice_fusion, f32[24,512]{1,0:T(8,128)S(1)} %get-tuple-element.111), kind=kOutput, calls=%fused_computation.264 | convolution fusion | flops 252653568 | bytes 15450152 | tf_op jit(solution)/shard_map/dot_general | solution.py:53
  195.8 3.4 collective-permute-start.17
  199.4 3.7 collective-permute-done.17
  205.3 3.4 collective-permute-start.18
  212.6 3.3 collective-permute-start.19
  220.7 11.8 %all-gather.4 = f32[96,512]{1,0:T(8,128)S(1)} all-gather(f32[24,512]{1,0:T(8,128)S(1)} %convolution_bitcast_fusion.5), channel_id=6, replica_groups=mesh['section'=8,'state'=4] {'state'}, dimensions={0}, use_global_device_ids=true | all-gather | bytes 245760 | tf_op jit(solution)/shard_map/all_gather | solution.py:15
  233.2 7.8 %subtract_multiply_fusion.5 = (f32[24,10,1024]{2,0,1:T(8,128)S(1)}, f32[24,10,1024]{2,0,1:T(8,128)S(1)}) fusion(f32[10]{0:T(128)S(1)} %copy-done.85, f32[49,12,1024]{2,0,1:T(8,128)} %copy-done.54, f32[24,10,1024]{2,0,1:T(8,128)} %copy-done.20, bf16[10,1024,512]{2,1,0:T(8,128)(2,1)} %constant_dynamic-update-slice_fusion, f32[24,512]{1,0:T(8,128)S(1)} %fusion.289), kind=kOutput, calls=%fused_computation.263 | convolution fusion | flops 252653568 | bytes 15450152 | tf_op jit(solution)/shard_map/dot_general | solution.py:53
  241.1 3.4 collective-permute-start.21
  244.7 3.7 collective-permute-done.21
  250.7 3.4 collective-permute-start.22
  258.0 3.3 collective-permute-start.23
  266.0 12.0 %all-gather.5 = f32[96,512]{1,0:T(8,128)} all-gather(f32[24,512]{1,0:T(8,128)S(1)} %convolution_bitcast_fusion.4), channel_id=7, replica_groups=mesh['section'=8,'state'=4] {'state'}, dimensions={0}, use_global_device_ids=true | all-gather | bytes 245760 | tf_op jit(solution)/shard_map/all_gather | solution.py:15
  281.7 7.8 %subtract_multiply_fusion.4 = (f32[24,10,1024]{2,0,1:T(8,128)S(1)}, f32[24,10,1024]{2,0,1:T(8,128)S(1)}) fusion(f32[10]{0:T(128)} %copy-done.83, f32[49,12,1024]{2,0,1:T(8,128)} %copy-done.51, f32[24,10,1024]{2,0,1:T(8,128)} %copy-done.14, bf16[10,1024,512]{2,1,0:T(8,128)(2,1)} %constant_dynamic-update-slice_fusion, f32[24,512]{1,0:T(8,128)S(1)} %get-tuple-element.117), kind=kOutput, calls=%fused_computation.262 | convolution fusion | flops 252653568 | bytes 15450152 | tf_op jit(solution)/shard_map/dot_general | solution.py:53
  289.6 3.4 collective-permute-start.25
  293.2 3.7 collective-permute-done.25
  299.2 3.8 collective-permute-start.26
  306.5 3.3 collective-permute-start.27
  314.6 11.6 %all-gather.6 = f32[96,512]{1,0:T(8,128)S(1)} all-gather(f32[24,512]{1,0:T(8,128)S(1)} %convolution_bitcast_fusion.3), channel_id=8, replica_groups=mesh['section'=8,'state'=4] {'state'}, dimensions={0}, use_global_device_ids=true | all-gather | bytes 245760 | tf_op jit(solution)/shard_map/all_gather | solution.py:15
  326.9 7.8 %subtract_multiply_fusion.3 = (f32[24,10,1024]{2,0,1:T(8,128)S(1)}, f32[24,10,1024]{2,0,1:T(8,128)S(1)}) fusion(f32[10]{0:T(128)S(1)} %copy-done.86, f32[49,12,1024]{2,0,1:T(8,128)} %copy-done.55, f32[24,10,1024]{2,0,1:T(8,128)} %copy-done.22, bf16[10,1024,512]{2,1,0:T(8,128)(2,1)} %constant_dynamic-update-slice_fusion, f32[24,512]{1,0:T(8,128)S(1)} %fusion.281), kind=kOutput, calls=%fused_computation.261 | convolution fusion | flops 252653568 | bytes 15450152 | tf_op jit(solution)/shard_map/dot_general | solution.py:53
  334.7 3.4 collective-permute-start.29
  338.3 3.7 collective-permute-done.29
  344.3 3.4 collective-permute-start.30
  351.6 3.3 collective-permute-start.31
  359.6 12.2 %all-gather.7 = f32[96,512]{1,0:T(8,128)} all-gather(f32[24,512]{1,0:T(8,128)S(1)} %convolution_bitcast_fusion.2), channel_id=9, replica_groups=mesh['section'=8,'state'=4] {'state'}, dimensions={0}, use_global_device_ids=true | all-gather | bytes 245760 | tf_op jit(solution)/shard_map/all_gather | solution.py:15
  375.5 7.8 %subtract_multiply_fusion.2 = (f32[24,10,1024]{2,0,1:T(8,128)S(1)}, f32[24,10,1024]{2,0,1:T(8,128)S(1)}) fusion(f32[10]{0:T(128)} %copy-done.83, f32[49,12,1024]{2,0,1:T(8,128)} %copy-done.52, f32[24,10,1024]{2,0,1:T(8,128)} %copy-done.16, bf16[10,1024,512]{2,1,0:T(8,128)(2,1)} %constant_dynamic-update-slice_fusion, f32[24,512]{1,0:T(8,128)S(1)} %get-tuple-element.123), kind=kOutput, calls=%fused_computation.260 | convolution fusion | flops 252653568 | bytes 15450152 | tf_op jit(solution)/shard_map/dot_general | solution.py:53
  383.4 3.4 collective-permute-start.33
  387.0 3.7 collective-permute-done.33
  392.9 3.4 collective-permute-start.34
  400.2 3.3 collective-permute-start.35
  408.3 11.6 %all-gather.8 = f32[96,512]{1,0:T(8,128)S(1)} all-gather(f32[24,512]{1,0:T(8,128)S(1)} %convolution_bitcast_fusion.1), channel_id=10, replica_groups=mesh['section'=8,'state'=4] {'state'}, dimensions={0}, use_global_device_ids=true | all-gather | bytes 245760 | tf_op jit(solution)/shard_map/all_gather | solution.py:15
  420.6 7.8 %subtract_multiply_fusion.1 = (f32[24,10,1024]{2,0,1:T(8,128)S(1)}, f32[24,10,1024]{2,0,1:T(8,128)S(1)}) fusion(f32[10]{0:T(128)S(1)} %copy-done.87, f32[49,12,1024]{2,0,1:T(8,128)} %copy-done.56, f32[24,10,1024]{2,0,1:T(8,128)} %copy-done.24, bf16[10,1024,512]{2,1,0:T(8,128)(2,1)} %constant_dynamic-update-slice_fusion, f32[24,512]{1,0:T(8,128)S(1)} %fusion.273), kind=kOutput, calls=%fused_computation.259 | convolution fusion | flops 252653568 | bytes 15450152 | tf_op jit(solution)/shard_map/dot_general | solution.py:53
  428.5 3.4 collective-permute-start.37
  432.1 3.7 collective-permute-done.37
  438.1 3.6 collective-permute-start.38
  445.4 3.3 collective-permute-start.39
  453.4 12.0 %all-gather.9 = f32[96,512]{1,0:T(8,128)} all-gather(f32[24,512]{1,0:T(8,128)S(1)} %convolution_bitcast_fusion), channel_id=11, replica_groups=mesh['section'=8,'state'=4] {'state'}, dimensions={0}, use_global_device_ids=true | all-gather | bytes 245760 | tf_op jit(solution)/shard_map/all_gather | solution.py:15
  466.9 3.1 multiply_reduce_fusion.12
  470.0 8.8 %subtract_multiply_fusion = (f32[24,10,1024]{2,0,1:T(8,128)S(1)}, f32[24,10,1024]{2,0,1:T(8,128)}) fusion(f32[10]{0:T(128)S(1)} %copy-done.88, f32[49,12,1024]{2,0,1:T(8,128)} %copy-done.57, f32[24,10,1024]{2,0,1:T(8,128)} %copy-done.26, bf16[10,1024,512]{2,1,0:T(8,128)(2,1)} %constant_dynamic-update-slice_fusion, bf16[24,512]{1,0:T(8,128)(2,1)S(1)} %get-tuple-element.128), kind=kOutput, calls=%fused_computation.258 | convolution fusion | flops 252641280 | bytes 15425576 | tf_op jit(solution)/shard_map/dot_general | solution.py:53
  478.8 3.3 collective-permute-start.41
  491.8 4.1 multiply_reduce_fusion
  498.8 43.1 %all-reduce.61 = (f32[]{:T(128)}, f32[]{:T(128)}, f32[]{:T(128)}, f32[]{:T(128)}, f32[]{:T(128)}, /*index=5*/f32[]{:T(128)}, f32[]{:T(128)}, f32[]{:T(128)}, f32...) all-reduce(f32[]{:T(128)S(6)} %div.131, ...), channel_id=1, replica_groups=mesh['section'=8,'state'=4] {'section','state'}, use_global_device_ids=true, to_apply=%region_13.14 | all-reduce | flops 20 | bytes 160 | tf_op jit(solution)/shard_map/psum | solution.py:117
  (473 shorter events, 142.0 us)
Async XLA Ops:
  0.6 35.4 %copy-start = (f32[512,512]{1,0:T(8,128)S(1)}, f32[512,512]{1,0:T(8,128)}, u32[]{:S(2)}) copy-start(f32[512,512]{1,0:T(8,128)} %param.10) | copy-start | bytes 3145732
  0.7 5.9 %collective-permute-start = (f32[8,1024]{1,0:T(8,128)S(1)}, f32[8,1024]{1,0:T(8,128)S(1)}, u32[]{:S(2)}, u32[]{:S(2)}) collective-permute-start(f32[8,1024]{1,0:T(8,128)S(1)} %squeeze.60), channel_id=1, source_target_pairs={{0,4},{4,8},{8,12},{12,16},{16,20},{20,24},{24,28},{1,5},{5,9},{9,... | collective-permute-start | bytes 98312 | tf_op jit(solution)/shard_map/ppermute | solution.py:36
  6.7 12.9 %collective-permute-start.2 = (f32[49,2,1024]{2,0,1:T(8,128)S(1)}, f32[49,2,1024]{2,0,1:T(8,128)S(1)}, u32[]{:S(2)}, u32[]{:S(2)}) collective-permute-start(f32[49,2,1024]{2,0,1:T(8,128)S(1)} %get-tuple-element.99), channel_id=1, source_target_pairs={{1,0},{2,1},{3,2},{5,4},{6,5},{7,6},{9,8},{10,9},{11,10},{13,12},{... | collective-permute-start | bytes 1204232 | tf_op jit(solution)/shard_map/ppermute | solution.py:28
  8.0 11.6 %collective-permute-start.1 = (f32[49,2,1024]{2,0,1:T(8,128)S(1)}, f32[49,2,1024]{2,0,1:T(8,128)S(1)}, u32[]{:S(2)}, u32[]{:S(2)}) collective-permute-start(f32[49,2,1024]{2,0,1:T(8,128)S(1)} %get-tuple-element.98), channel_id=1, source_target_pairs={{0,1},{1,2},{2,3},{4,5},{5,6},{6,7},{8,9},{9,10},{10,11},{12,13},{... | collective-permute-start | bytes 1204232 | tf_op jit(solution)/shard_map/ppermute | solution.py:25
  14.1 22.6 %collective-permute-start.3 = (bf16[1,1024,512]{2,1,0:T(8,128)(2,1)}, bf16[1,1024,512]{2,1,0:T(8,128)(2,1)}, u32[]{:S(2)}, u32[]{:S(2)}) collective-permute-start(bf16[1,1024,512]{2,1,0:T(8,128)(2,1)} %get-tuple-element.77), channel_id=1, source_target_pairs={{0,1},{1,2},{2,3},{4,5},{5,6},{6,7},{8,9},{9,10},{10,11},{12,13},{... | collective-permute-start | bytes 3145736 | tf_op jit(solution)/shard_map/ppermute | solution.py:25
  18.1 28.2 %collective-permute-start.4 = (bf16[1,1024,512]{2,1,0:T(8,128)(2,1)}, bf16[1,1024,512]{2,1,0:T(8,128)(2,1)}, u32[]{:S(2)}, u32[]{:S(2)}) collective-permute-start(bf16[1,1024,512]{2,1,0:T(8,128)(2,1)} %get-tuple-element.76), channel_id=1, source_target_pairs={{1,0},{2,1},{3,2},{5,4},{6,5},{7,6},{9,8},{10,9},{11,10},{13,12},{... | collective-permute-start | bytes 3145736 | tf_op jit(solution)/shard_map/ppermute | solution.py:28
  19.4 29.1 %copy-start.83 = (f32[10]{0:T(128)}, f32[10]{0:T(128)S(1)}, u32[]{:S(2)}) copy-start(f32[10]{0:T(128)S(1)} %or_select_fusion) | copy-start | bytes 124
  21.6 27.0 %copy-start.46 = (f32[24,10,1024]{2,0,1:T(8,128)}, f32[24,10,1024]{2,0,1:T(8,128)S(1)}, u32[]{:S(2)}) copy-start(f32[24,10,1024]{2,0,1:T(8,128)S(1)} %fusion.5) | copy-start | bytes 2949124
  56.2 7.3 %collective-permute-start.5 = (f32[10,1024]{1,0:T(8,128)S(1)}, f32[10,1024]{1,0:T(8,128)S(1)}, u32[]{:S(2)}, u32[]{:S(2)}) collective-permute-start(f32[10,1024]{1,0:T(8,128)S(1)} %bitcast.265), channel_id=1, source_target_pairs={{4,0},{8,4},{12,8},{16,12},{20,16},{24,20},{28,24},{5,1},{9,5},{13... | collective-permute-start | bytes 122888 | tf_op jit(solution)/shard_map/ppermute | solution.py:36
  63.6 16.2 %slice-start = ((s8[8388608]{0:T(1024)(128)(4,1)}), s8[4194304]{0:T(1024)(128)(4,1)S(1)}, s32[]{:S(2)}) async-start(s8[8388608]{0:T(1024)(128)(4,1)} %bitcast.236), calls=%async_computation | async-start | bytes 8388608
  66.0 5.8 %collective-permute-start.6 = (f32[8,1024]{1,0:T(8,128)S(1)}, f32[8,1024]{1,0:T(8,128)S(1)}, u32[]{:S(2)}, u32[]{:S(2)}) collective-permute-start(f32[8,1024]{1,0:T(8,128)S(1)} %bitcast.291), channel_id=1, source_target_pairs={{0,4},{4,8},{8,12},{12,16},{16,20},{20,24},{24,28},{1,5},{5,9},{9,... | collective-permute-start | bytes 98312 | tf_op jit(solution)/shard_map/ppermute | solution.py:36
  72.0 4.4 collective-permute-start.8
  73.3 4.5 collective-permute-start.7
  102.3 7.3 %collective-permute-start.9 = (f32[10,1024]{1,0:T(8,128)S(1)}, f32[10,1024]{1,0:T(8,128)S(1)}, u32[]{:S(2)}, u32[]{:S(2)}) collective-permute-start(f32[10,1024]{1,0:T(8,128)S(1)} %bitcast.267), channel_id=1, source_target_pairs={{4,0},{8,4},{12,8},{16,12},{20,16},{24,20},{28,24},{5,1},{9,5},{13... | collective-permute-start | bytes 122888 | tf_op jit(solution)/shard_map/ppermute | solution.py:36
  111.9 5.8 %collective-permute-start.10 = (f32[8,1024]{1,0:T(8,128)S(1)}, f32[8,1024]{1,0:T(8,128)S(1)}, u32[]{:S(2)}, u32[]{:S(2)}) collective-permute-start(f32[8,1024]{1,0:T(8,128)S(1)} %bitcast.283), channel_id=1, source_target_pairs={{0,4},{4,8},{8,12},{12,16},{16,20},{20,24},{24,28},{1,5},{5,9},{9,... | collective-permute-start | bytes 98312 | tf_op jit(solution)/shard_map/ppermute | solution.py:36
  117.9 4.6 collective-permute-start.12
  119.2 4.7 collective-permute-start.11
  126.0 12.9 %copy-start.61 = (f32[24,512]{1,0:T(8,128)S(1)}, f32[24,512]{1,0:T(8,128)}, u32[]{:S(2)}) copy-start(f32[24,512]{1,0:T(8,128)} %get-tuple-element.104) | copy-start | bytes 147460
  126.0 12.8 %copy-start.72 = (f32[24,512]{1,0:T(8,128)S(1)}, f32[24,512]{1,0:T(8,128)}, u32[]{:S(2)}) copy-start(f32[24,512]{1,0:T(8,128)} %copy-done.71) | copy-start | bytes 147460
  126.1 13.5 %copy-start.84 = (f32[10]{0:T(128)S(1)}, f32[10]{0:T(128)}, u32[]{:S(2)}) copy-start(f32[10]{0:T(128)} %copy-done.83) | copy-start | bytes 124
  147.4 7.3 %collective-permute-start.13 = (f32[10,1024]{1,0:T(8,128)S(1)}, f32[10,1024]{1,0:T(8,128)S(1)}, u32[]{:S(2)}, u32[]{:S(2)}) collective-permute-start(f32[10,1024]{1,0:T(8,128)S(1)} %bitcast.269), channel_id=1, source_target_pairs={{4,0},{8,4},{12,8},{16,12},{20,16},{24,20},{28,24},{5,1},{9,5},{13... | collective-permute-start | bytes 122888 | tf_op jit(solution)/shard_map/ppermute | solution.py:36
  156.9 5.8 %collective-permute-start.14 = (f32[8,1024]{1,0:T(8,128)S(1)}, f32[8,1024]{1,0:T(8,128)S(1)}, u32[]{:S(2)}, u32[]{:S(2)}) collective-permute-start(f32[8,1024]{1,0:T(8,128)S(1)} %bitcast.284), channel_id=1, source_target_pairs={{0,4},{4,8},{8,12},{12,16},{16,20},{20,24},{24,28},{1,5},{5,9},{9,... | collective-permute-start | bytes 98312 | tf_op jit(solution)/shard_map/ppermute | solution.py:36
  162.9 4.6 collective-permute-start.16
  164.2 4.7 collective-permute-start.15
  195.8 7.3 %collective-permute-start.17 = (f32[10,1024]{1,0:T(8,128)S(1)}, f32[10,1024]{1,0:T(8,128)S(1)}, u32[]{:S(2)}, u32[]{:S(2)}) collective-permute-start(f32[10,1024]{1,0:T(8,128)S(1)} %bitcast.271), channel_id=1, source_target_pairs={{4,0},{8,4},{12,8},{16,12},{20,16},{24,20},{28,24},{5,1},{9,5},{13... | collective-permute-start | bytes 122888 | tf_op jit(solution)/shard_map/ppermute | solution.py:36
  205.3 5.8 %collective-permute-start.18 = (f32[8,1024]{1,0:T(8,128)S(1)}, f32[8,1024]{1,0:T(8,128)S(1)}, u32[]{:S(2)}, u32[]{:S(2)}) collective-permute-start(f32[8,1024]{1,0:T(8,128)S(1)} %bitcast.285), channel_id=1, source_target_pairs={{0,4},{4,8},{8,12},{12,16},{16,20},{20,24},{24,28},{1,5},{5,9},{9,... | collective-permute-start | bytes 98312 | tf_op jit(solution)/shard_map/ppermute | solution.py:36
  211.3 4.6 collective-permute-start.20
  212.6 4.7 collective-permute-start.19
  219.4 13.1 %copy-start.62 = (f32[24,512]{1,0:T(8,128)S(1)}, f32[24,512]{1,0:T(8,128)}, u32[]{:S(2)}) copy-start(f32[24,512]{1,0:T(8,128)} %get-tuple-element.104) | copy-start | bytes 147460
  219.4 13.1 %copy-start.67 = (f32[24,512]{1,0:T(8,128)S(1)}, f32[24,512]{1,0:T(8,128)}, u32[]{:S(2)}) copy-start(f32[24,512]{1,0:T(8,128)} %get-tuple-element.110) | copy-start | bytes 147460
  219.5 13.1 %copy-start.74 = (f32[24,512]{1,0:T(8,128)S(1)}, f32[24,512]{1,0:T(8,128)}, u32[]{:S(2)}) copy-start(f32[24,512]{1,0:T(8,128)} %copy-done.73) | copy-start | bytes 147460
  219.5 13.7 %copy-start.85 = (f32[10]{0:T(128)S(1)}, f32[10]{0:T(128)}, u32[]{:S(2)}) copy-start(f32[10]{0:T(128)} %copy-done.83) | copy-start | bytes 124
  241.1 7.3 %collective-permute-start.21 = (f32[10,1024]{1,0:T(8,128)S(1)}, f32[10,1024]{1,0:T(8,128)S(1)}, u32[]{:S(2)}, u32[]{:S(2)}) collective-permute-start(f32[10,1024]{1,0:T(8,128)S(1)} %bitcast.273), channel_id=1, source_target_pairs={{4,0},{8,4},{12,8},{16,12},{20,16},{24,20},{28,24},{5,1},{9,5},{13... | collective-permute-start | bytes 122888 | tf_op jit(solution)/shard_map/ppermute | solution.py:36
  250.7 5.8 %collective-permute-start.22 = (f32[8,1024]{1,0:T(8,128)S(1)}, f32[8,1024]{1,0:T(8,128)S(1)}, u32[]{:S(2)}, u32[]{:S(2)}) collective-permute-start(f32[8,1024]{1,0:T(8,128)S(1)} %bitcast.286), channel_id=1, source_target_pairs={{0,4},{4,8},{8,12},{12,16},{16,20},{20,24},{24,28},{1,5},{5,9},{9,... | collective-permute-start | bytes 98312 | tf_op jit(solution)/shard_map/ppermute | solution.py:36
  256.7 4.6 collective-permute-start.24
  258.0 4.7 collective-permute-start.23
  289.6 7.3 %collective-permute-start.25 = (f32[10,1024]{1,0:T(8,128)S(1)}, f32[10,1024]{1,0:T(8,128)S(1)}, u32[]{:S(2)}, u32[]{:S(2)}) collective-permute-start(f32[10,1024]{1,0:T(8,128)S(1)} %bitcast.275), channel_id=1, source_target_pairs={{4,0},{8,4},{12,8},{16,12},{20,16},{24,20},{28,24},{5,1},{9,5},{13... | collective-permute-start | bytes 122888 | tf_op jit(solution)/shard_map/ppermute | solution.py:36
  299.2 5.8 %collective-permute-start.26 = (f32[8,1024]{1,0:T(8,128)S(1)}, f32[8,1024]{1,0:T(8,128)S(1)}, u32[]{:S(2)}, u32[]{:S(2)}) collective-permute-start(f32[8,1024]{1,0:T(8,128)S(1)} %bitcast.287), channel_id=1, source_target_pairs={{0,4},{4,8},{8,12},{12,16},{16,20},{20,24},{24,28},{1,5},{5,9},{9,... | collective-permute-start | bytes 98312 | tf_op jit(solution)/shard_map/ppermute | solution.py:36
  305.2 4.6 collective-permute-start.28
  306.5 4.7 collective-permute-start.27
  313.3 12.9 %copy-start.64 = (f32[24,512]{1,0:T(8,128)S(1)}, f32[24,512]{1,0:T(8,128)}, u32[]{:S(2)}) copy-start(f32[24,512]{1,0:T(8,128)} %copy-done.63) | copy-start | bytes 147460
  313.3 12.9 %copy-start.68 = (f32[24,512]{1,0:T(8,128)S(1)}, f32[24,512]{1,0:T(8,128)}, u32[]{:S(2)}) copy-start(f32[24,512]{1,0:T(8,128)} %get-tuple-element.110) | copy-start | bytes 147460
  313.3 12.9 %copy-start.69 = (f32[24,512]{1,0:T(8,128)S(1)}, f32[24,512]{1,0:T(8,128)}, u32[]{:S(2)}) copy-start(f32[24,512]{1,0:T(8,128)} %get-tuple-element.116) | copy-start | bytes 147460
  313.3 12.9 %copy-start.76 = (f32[24,512]{1,0:T(8,128)S(1)}, f32[24,512]{1,0:T(8,128)}, u32[]{:S(2)}) copy-start(f32[24,512]{1,0:T(8,128)} %copy-done.75) | copy-start | bytes 147460
  313.3 13.5 %copy-start.86 = (f32[10]{0:T(128)S(1)}, f32[10]{0:T(128)}, u32[]{:S(2)}) copy-start(f32[10]{0:T(128)} %copy-done.83) | copy-start | bytes 124
  334.7 7.3 %collective-permute-start.29 = (f32[10,1024]{1,0:T(8,128)S(1)}, f32[10,1024]{1,0:T(8,128)S(1)}, u32[]{:S(2)}, u32[]{:S(2)}) collective-permute-start(f32[10,1024]{1,0:T(8,128)S(1)} %bitcast.277), channel_id=1, source_target_pairs={{4,0},{8,4},{12,8},{16,12},{20,16},{24,20},{28,24},{5,1},{9,5},{13... | collective-permute-start | bytes 122888 | tf_op jit(solution)/shard_map/ppermute | solution.py:36
  344.3 5.8 %collective-permute-start.30 = (f32[8,1024]{1,0:T(8,128)S(1)}, f32[8,1024]{1,0:T(8,128)S(1)}, u32[]{:S(2)}, u32[]{:S(2)}) collective-permute-start(f32[8,1024]{1,0:T(8,128)S(1)} %bitcast.288), channel_id=1, source_target_pairs={{0,4},{4,8},{8,12},{12,16},{16,20},{20,24},{24,28},{1,5},{5,9},{9,... | collective-permute-start | bytes 98312 | tf_op jit(solution)/shard_map/ppermute | solution.py:36
  350.3 4.6 collective-permute-start.32
  351.6 4.7 collective-permute-start.31
  383.4 7.3 %collective-permute-start.33 = (f32[10,1024]{1,0:T(8,128)S(1)}, f32[10,1024]{1,0:T(8,128)S(1)}, u32[]{:S(2)}, u32[]{:S(2)}) collective-permute-start(f32[10,1024]{1,0:T(8,128)S(1)} %bitcast.279), channel_id=1, source_target_pairs={{4,0},{8,4},{12,8},{16,12},{20,16},{24,20},{28,24},{5,1},{9,5},{13... | collective-permute-start | bytes 122888 | tf_op jit(solution)/shard_map/ppermute | solution.py:36
  392.9 5.8 %collective-permute-start.34 = (f32[8,1024]{1,0:T(8,128)S(1)}, f32[8,1024]{1,0:T(8,128)S(1)}, u32[]{:S(2)}, u32[]{:S(2)}) collective-permute-start(f32[8,1024]{1,0:T(8,128)S(1)} %bitcast.289), channel_id=1, source_target_pairs={{0,4},{4,8},{8,12},{12,16},{16,20},{20,24},{24,28},{1,5},{5,9},{9,... | collective-permute-start | bytes 98312 | tf_op jit(solution)/shard_map/ppermute | solution.py:36
  398.9 4.6 collective-permute-start.36
  400.2 4.7 collective-permute-start.35
  407.0 12.9 %copy-start.66 = (f32[24,512]{1,0:T(8,128)S(1)}, f32[24,512]{1,0:T(8,128)}, u32[]{:S(2)}) copy-start(f32[24,512]{1,0:T(8,128)} %copy-done.65) | copy-start | bytes 147460
  407.1 12.9 %copy-start.70 = (f32[24,512]{1,0:T(8,128)S(1)}, f32[24,512]{1,0:T(8,128)}, u32[]{:S(2)}) copy-start(f32[24,512]{1,0:T(8,128)} %get-tuple-element.116) | copy-start | bytes 147460
  407.1 12.9 %copy-start.78 = (f32[24,512]{1,0:T(8,128)S(1)}, f32[24,512]{1,0:T(8,128)}, u32[]{:S(2)}) copy-start(f32[24,512]{1,0:T(8,128)} %copy-done.77) | copy-start | bytes 147460
  407.1 12.9 %copy-start.81 = (f32[24,512]{1,0:T(8,128)S(1)}, f32[24,512]{1,0:T(8,128)}, u32[]{:S(2)}) copy-start(f32[24,512]{1,0:T(8,128)} %get-tuple-element.122) | copy-start | bytes 147460
  407.1 13.5 %copy-start.87 = (f32[10]{0:T(128)S(1)}, f32[10]{0:T(128)}, u32[]{:S(2)}) copy-start(f32[10]{0:T(128)} %copy-done.83) | copy-start | bytes 124
  428.5 7.3 %collective-permute-start.37 = (f32[10,1024]{1,0:T(8,128)S(1)}, f32[10,1024]{1,0:T(8,128)S(1)}, u32[]{:S(2)}, u32[]{:S(2)}) collective-permute-start(f32[10,1024]{1,0:T(8,128)S(1)} %bitcast.281), channel_id=1, source_target_pairs={{4,0},{8,4},{12,8},{16,12},{20,16},{24,20},{28,24},{5,1},{9,5},{13... | collective-permute-start | bytes 122888 | tf_op jit(solution)/shard_map/ppermute | solution.py:36
  438.1 5.8 %collective-permute-start.38 = (f32[8,1024]{1,0:T(8,128)S(1)}, f32[8,1024]{1,0:T(8,128)S(1)}, u32[]{:S(2)}, u32[]{:S(2)}) collective-permute-start(f32[8,1024]{1,0:T(8,128)S(1)} %bitcast.290), channel_id=1, source_target_pairs={{0,4},{4,8},{8,12},{12,16},{16,20},{20,24},{24,28},{1,5},{5,9},{9,... | collective-permute-start | bytes 98312 | tf_op jit(solution)/shard_map/ppermute | solution.py:36
  444.1 4.6 collective-permute-start.40
  445.4 4.7 collective-permute-start.39
  452.1 17.9 %copy-start.88 = (f32[10]{0:T(128)S(1)}, f32[10]{0:T(128)}, u32[]{:S(2)}) copy-start(f32[10]{0:T(128)} %copy-done.83) | copy-start | bytes 124
  478.8 10.8 %collective-permute-start.41 = (f32[10,1024]{1,0:T(8,128)S(1)}, f32[10,1024]{1,0:T(8,128)}, u32[]{:S(2)}, u32[]{:S(2)}) collective-permute-start(f32[10,1024]{1,0:T(8,128)S(1)} %bitcast.264), channel_id=1, source_target_pairs={{4,0},{8,4},{12,8},{16,12},{20,16},{24,20},{28,24},{5,1},{9,5},{13... | collective-permute-start | bytes 122888 | tf_op jit(solution)/shard_map/ppermute | solution.py:36
  (85 other events, 553.1 us)
